TPU v7x, 256 devices: a whole 4x4x8 slice. The times are simulated.
256 devices in a mesh: ctx: 64 (over x, z, core), head: 4 (over y).
Axes of the slice: x: 4, y: 4, z: 8, core: 2. Of those that a mesh axis runs over, the one named last changes fastest.
Arguments:
- queries: bfloat16 [16384, 2048], P(('ctx', 'head')), may hold values from -6 to 6
- key_vectors_state: bfloat16 [16384, 512], P(('ctx', 'head')), may hold values from -6 to 6
- value_vectors_state: bfloat16 [16384, 512], P(('ctx', 'head')), may hold values from -6 to 6
- doc_bounds: int32 [17], replicated, may hold values from 0 to 16384, as said below
Outputs:
- attended: bfloat16 [16384, 2048], P(('ctx', 'head'))
Inputs may be any that keep to these rules, and one draw needn't show every extreme that they name: doc_bounds[0] is 0 and doc_bounds[16] is 16384; the entries strictly increase, and doc_bounds[1] to doc_bounds[15] all lie below 8192, so the last document holds at least half of the tokens.
All inputs are finite; a program needn't handle non-finite values.
Results may differ from a plain program's by a relative error of at most 0.004.
Values may be sent and summed in bfloat16 or wider, within the bound.
No kernel may reach another device: no remote copies, remote signals or barrier semaphores. Data moves between devices by JAX's collectives and lax.ppermute only.
A program may use at most 64 MiB of HBM per device.

v0:
```python
import functools
import math

import jax
import jax.numpy as jnp
from jax import lax
from jax.experimental import pallas as pl
from jax.experimental.pallas import tpu as pltpu
from jax.sharding import Mesh, PartitionSpec as P


QUERY_HEADS = 32
KEY_VALUE_HEADS = 8
HEAD_SIZE = 64
DOCS = 16
GROUP = QUERY_HEADS // KEY_VALUE_HEADS

X, Z, CORES, Y = 4, 8, 2, 4
AXES = ("x", "z", "core", "y")
BLOCK = 64
TILE = Y * BLOCK
SPAN = CORES * TILE
PAIR = 2
PAIRS = Z // PAIR
PLANE = Z * SPAN
STRIDE = PAIR * SPAN
HALF = GROUP * BLOCK
ROWS = PAIR * HALF
KEYS = PAIR * TILE
WIDE = 2 * HEAD_SIZE
HEAD_COLS = GROUP * HEAD_SIZE
BASE = (3, 1, 0, 2)
BLOCKS = X * PAIRS
NEVER = 1 << 20

EXP2_SCALE = math.log2(math.e) / math.sqrt(HEAD_SIZE)
START_MAX = -1e30
HIDDEN = -3e38
LARGEST_SUM = 2.0 ** 60


def square_groups():
    groups = []
    for k in range(X):
        for core in range(CORES):
            for y in range(Y):
                groups.append([(((BASE[z // PAIR] ^ k) * Z + z) * CORES + core) * Y + y for z in range(Z)])
    return groups


def base_of(pair):
    base = jnp.int32(BASE[-1])
    for p in range(PAIRS - 1):
        base = jnp.where(pair == p, BASE[p], base)
    return base


def line_groups(first):
    index = lambda x, z, core, y: ((x * Z + z) * CORES + core) * Y + y
    groups = []
    for z in range(Z):
        for core in range(CORES):
            if (core == 0) == first:
                groups += [[index(x, z, core, y) for x in range(X)] for y in range(Y)]
            else:
                groups += [[index(x, z, core, y) for y in range(Y)] for x in range(X)]
    return groups


def doc_start(bounds, position):
    start = jnp.zeros_like(position)
    for d in range(1, DOCS):
        start = jnp.where(bounds[d] <= position, bounds[d], start)
    return start


def mix(values, weights):
    return jnp.dot(values, weights.astype(jnp.bfloat16), preferred_element_type=jnp.float32)


def start_kernel(bounds, q_ref, rows_ref, top_ref, acc_ref):
    x, z, core, y = (lax.axis_index(a) for a in AXES)
    group = x ^ base_of(lax.div(z, PAIR))
    column = lax.broadcasted_iota(jnp.int32, (1, WIDE), 1)
    key_lanes = (column < HEAD_SIZE).astype(jnp.bfloat16)
    value_lanes = (column >= HEAD_SIZE).astype(jnp.bfloat16)
    row = lax.broadcasted_iota(jnp.int32, (1, ROWS), 1)
    row_offset = lax.div(row, HALF) * SPAN + lax.rem(row, BLOCK)

    def one_pair(p, _):
        first = (base_of(p) ^ group) * PLANE + p * STRIDE + core * TILE + y * BLOCK
        line = lax.broadcasted_iota(jnp.int32, (HEAD_SIZE, ROWS), 0)
        half = lax.broadcasted_iota(jnp.int32, (HEAD_SIZE, ROWS), 1) // HALF
        filler = ((line == 0) | (line == half + 1)).astype(jnp.bfloat16)
        own = [q_ref[PAIR * p + b] for b in range(PAIR)]
        pieces = []
        for block in own:
            turned = block[:, WIDE:].T
            pieces += [turned[j * HEAD_SIZE:(j + 1) * HEAD_SIZE] for j in range(GROUP)]
        rows = jnp.concatenate([jnp.concatenate(pieces, axis=1), filler], axis=0)
        rows_ref[p] = rows
        kv = jnp.concatenate([block[:, :WIDE] for block in own], axis=0)
        k = lax.broadcasted_iota(jnp.int32, (PAIR * BLOCK, 1), 0)
        k_offset = lax.div(k, BLOCK) * SPAN + lax.rem(k, BLOCK)
        scores = jnp.dot(kv * key_lanes, rows, preferred_element_type=jnp.float32)
        lo = doc_start(bounds, first + row_offset) - first
        scores = jnp.where((k_offset >= lo) & (k_offset <= row_offset), scores, HIDDEN)
        top = jnp.max(scores, axis=0, keepdims=True)
        top_ref[p] = top
        acc_ref[p] = mix((kv * value_lanes + key_lanes).T, jnp.exp2(scores * EXP2_SCALE - top * EXP2_SCALE))
        return 0

    lax.fori_loop(0, PAIRS, one_pair, 0)


def attention_kernel(stage, bounds, *refs):
    if stage == 0:
        rows_ref, top_ref, acc_in, own_ref, acc_out = refs
    else:
        rows_ref, top_ref, acc_in, own_ref, other_ref, out_ref, acc_ref, run_ref = refs
    x, z, core, y = (lax.axis_index(a) for a in AXES)
    mine = base_of(lax.div(z, PAIR))
    group = x ^ mine
    column = lax.broadcasted_iota(jnp.int32, (1, WIDE), 1)
    key_lanes = (column < HEAD_SIZE).astype(jnp.bfloat16)
    value_lanes = (column >= HEAD_SIZE).astype(jnp.bfloat16)
    row = lax.broadcasted_iota(jnp.int32, (1, ROWS), 1)
    row_offset = lax.div(row, HALF) * SPAN + lax.rem(row, BLOCK)
    key = lax.broadcasted_iota(jnp.int32, (KEYS, WIDE), 0)
    key_offset = lax.div(key, TILE) * SPAN + lax.rem(key, TILE)
    kv_ref, offset = (own_ref, core) if stage == 0 else (other_ref, 1 - core)

    def one_pair(p, _):
        plane = base_of(p) ^ group
        home = plane * PAIRS + p
        first = home * STRIDE + core * TILE + y * BLOCK
        start = doc_start(bounds, first)
        begin = lax.div(start, STRIDE)
        one_document = start == doc_start(bounds, first + SPAN + BLOCK - 1)

        after = jnp.where(column == HEAD_SIZE + 1, first, jnp.where(column == HEAD_SIZE + 2, first + SPAN, NEVER))
        held = jnp.where(column == HEAD_SIZE, first, NEVER)

        def load(kv_ref, offset, blocks, limits=None):
            parts, masks, origins = [], [], []
            for n, block in enumerate(blocks):
                near = jnp.minimum(block, BLOCKS - 1)
                q = lax.rem(near, PAIRS)
                source = lax.div(near, PAIRS) ^ base_of(q) ^ mine
                for g in range(PAIR):
                    for i in range(Y):
                        at = jnp.where(offset == 0, i * X + source, source * Y + i)
                        parts.append(kv_ref[at, q * PAIR + g])
                origin = block * STRIDE + offset * TILE
                origins.append(origin)
                if limits is not None:
                    before = jnp.where(column == HEAD_SIZE, limits[n] - origin, -NEVER)
                    unseen = (key_offset < before) | (key_offset >= after - origin)
                    if stage == 0:
                        unseen = unseen | ((key_offset >= held - origin) & (key_offset < held + BLOCK - origin))
                    masks.append(jnp.where(unseen, START_MAX, 0.0))
            kv = jnp.concatenate(parts, axis=0)
            keys = kv * key_lanes
            if limits is not None:
                keys = keys + jnp.concatenate(masks, axis=0).astype(jnp.bfloat16)
            return keys, (kv * value_lanes + key_lanes).T, origins

        def across(origins, low, high=None):
            offsets = jnp.concatenate([key_offset] * (ROWS // WIDE), axis=1)
            seen = []
            for origin in origins:
                inside = offsets >= low - origin
                seen.append(inside if high is None else inside & (offsets <= high - origin))
            return seen

        def hide(scores, seen):
            parts = [jnp.where(m, scores[n * KEYS:(n + 1) * KEYS], HIDDEN) for n, m in enumerate(seen)]
            return jnp.concatenate(parts, axis=0)

        if stage == 0:
            acc = acc_out.at[p]
        else:
            acc = acc_ref
        acc[...] = acc_in[p]

        def add(blocks, limits=None, lo=None):
            keys, values, origins = load(kv_ref, offset, blocks, limits)
            scores = jnp.dot(keys, rows_ref[p], preferred_element_type=jnp.float32)
            if lo is not None:
                scores = hide(scores, across(origins, lo))
            weights = jnp.exp2(scores * EXP2_SCALE - top_ref[p] * EXP2_SCALE)
            acc[...] += mix(values, weights)

        @pl.when(one_document)
        def _():
            add([home, begin], [start, jnp.where(begin == home, NEVER, start)])
            inside = home - begin - 1

            def step(s, _):
                add([begin + 1 + 4 * s + n for n in range(4)])
                return 0

            lax.fori_loop(0, lax.div(inside, 4), step, 0)

            @pl.when((inside > 0) & (lax.rem(inside, 4) >= 2))
            def _():
                left = begin + 1 + inside - lax.rem(inside, 4)
                add([left, left + 1])

            @pl.when((inside > 0) & (lax.rem(inside, 2) == 1))
            def _():
                add([home - 1])

        @pl.when(jnp.logical_not(one_document))
        def _():
            lo = doc_start(bounds, first + row_offset)

            count = home - begin + 1

            def step(s, _):
                add([begin + 2 * s, begin + 2 * s + 1], [start, start], lo)
                return 0

            lax.fori_loop(0, lax.div(count, 2), step, 0)

            @pl.when(lax.rem(count, 2) == 1)
            def _():
                add([home], [start], lo)

        if stage == 0:
            return 0

        within = jnp.min((acc[0:1, :] <= LARGEST_SUM).astype(jnp.float32))

        @pl.when(within < 0.5)
        def _():
            hi = first + row_offset
            lo = doc_start(bounds, hi)
            acc[...] = jnp.zeros_like(acc)
            run_ref[...] = jnp.full(run_ref.shape, START_MAX, jnp.float32)
            for again_ref, again_offset in ((own_ref, core), (other_ref, 1 - core)):
                def step(block, _):
                    keys, values, origins = load(again_ref, again_offset, [block])
                    scores = jnp.dot(keys, rows_ref[p], preferred_element_type=jnp.float32)
                    scores = hide(scores, across(origins, lo, hi))
                    top = run_ref[...]
                    new_top = jnp.maximum(top, jnp.max(scores, axis=0, keepdims=True))
                    shrink = jnp.exp2((top - new_top) * EXP2_SCALE)
                    acc[...] = acc[...] * shrink + mix(values, jnp.exp2((scores - new_top) * EXP2_SCALE))
                    run_ref[...] = new_top
                    return 0

                lax.fori_loop(begin, home + 1, step, 0)

        result = (acc[HEAD_SIZE:, :] / acc[0:1, :]).T
        for b in range(PAIR):
            heads = [result[(b * GROUP + j) * BLOCK:(b * GROUP + j + 1) * BLOCK] for j in range(GROUP)]
            out_ref[PAIR * p + b] = jnp.concatenate(heads, axis=1).astype(jnp.bfloat16)
        return 0

    lax.fori_loop(0, PAIRS, one_pair, 0)


def pack_kernel(q_ref, k_ref, v_ref, out_ref):
    for h in range(KEY_VALUE_HEADS):
        cols = slice(h * HEAD_SIZE, (h + 1) * HEAD_SIZE)
        out_ref[h, :, :WIDE] = jnp.concatenate([k_ref[:, cols], v_ref[:, cols]], axis=1)
        out_ref[h, :, WIDE:] = q_ref[:, h * HEAD_COLS:(h + 1) * HEAD_COLS]


def on_device(queries, keys, values, doc_bounds):
    smem = pl.BlockSpec(memory_space=pltpu.SMEM)
    vmem = pl.BlockSpec(memory_space=pltpu.VMEM)
    groups = square_groups()
    packed = pl.pallas_call(
        pack_kernel,
        out_shape=pltpu.VMEM((Z, BLOCK, WIDE + HEAD_COLS), jnp.bfloat16),
        in_specs=[vmem] * 3,
        out_specs=vmem,
        name="pack",
    )(queries, keys, values)
    packed = lax.all_to_all(packed, AXES, 0, 0, axis_index_groups=groups, tiled=True)
    gathered = packed[:, :, :WIDE]
    for first in (True, False):
        copies = jnp.broadcast_to(gathered[None], (X,) + gathered.shape)
        gathered = lax.all_to_all(copies, AXES, 0, 0, axis_index_groups=line_groups(first), tiled=True)
    own = gathered.reshape(X * Y, Z, BLOCK, WIDE)
    other = lax.ppermute(own, "core", [(0, 1), (1, 0)])

    acc_shape = jax.ShapeDtypeStruct((PAIRS, WIDE, ROWS), jnp.float32)
    top_shape = jax.ShapeDtypeStruct((PAIRS, 1, ROWS), jnp.float32)
    rows_shape = jax.ShapeDtypeStruct((PAIRS, WIDE, ROWS), jnp.bfloat16)
    params = pltpu.CompilerParams(vmem_limit_bytes=40 * 1024 * 1024)
    rows, top, acc = pl.pallas_call(
        start_kernel,
        out_shape=tuple(pltpu.VMEM(a.shape, a.dtype) for a in (rows_shape, top_shape, acc_shape)),
        in_specs=[smem, vmem],
        out_specs=(vmem,) * 3,
        name="attention_start",
    )(doc_bounds, packed)
    acc = pl.pallas_call(
        functools.partial(attention_kernel, 0),
        out_shape=acc_shape,
        in_specs=[smem] + [vmem] * 4,
        out_specs=vmem,
        compiler_params=params,
        name="attention_own",
    )(doc_bounds, rows, top, acc, own)
    attended = pl.pallas_call(
        functools.partial(attention_kernel, 1),
        out_shape=jax.ShapeDtypeStruct((Z, BLOCK, HEAD_COLS), jnp.bfloat16),
        in_specs=[smem] + [vmem] * 5,
        out_specs=vmem,
        scratch_shapes=[pltpu.VMEM((WIDE, ROWS), jnp.float32), pltpu.VMEM((1, ROWS), jnp.float32)],
        compiler_params=params,
        name="attention_other",
    )(doc_bounds, rows, top, acc, own, other)
    attended = lax.all_to_all(attended, AXES, 0, 0, axis_index_groups=groups, tiled=True)
    return attended.transpose(1, 0, 2).reshape(BLOCK, QUERY_HEADS * HEAD_SIZE)


def solution(mesh):
    split = Mesh(mesh.devices.reshape(X, Z, CORES, Y), AXES)
    rows = P(AXES, None)
    return jax.shard_map(
        on_device,
        mesh=split,
        in_specs=(rows, rows, rows, P()),
        out_specs=rows,
        check_vma=False,
    )
```

profile of v0, /device:TPU:6, one launch (start us, length us, event | category | flops | bytes accessed | tf_op | source)
XLA Modules:
  0.0 96.4 jit_solution(1688386339615764473)
XLA Ops:
  0.0 1.1 %pack.1 = bf16[8,64,384]{2,1,0:T(8,128)(2,1)S(1)} custom-call(bf16[64,2048]{1,0:T(8,128)(2,1)} %q_ref.1, bf16[64,512]{1,0:T(8,128)(2,1)} %k_ref.1, bf16[64,512]{1,0:T(8,128)(2,1)} %v_ref.1), custom_call_target="tpu_custom_call" | custom-call | tf_op jit(solution)/shard_map/pack/pallas_call | solution.py:275
  1.1 24.4 %all_to_all.20.q_ref = bf16[8,64,384]{2,1,0:T(8,128)(2,1)S(1)} all-to-all(bf16[8,64,384]{2,1,0:T(8,128)(2,1)S(1)} %pack.1), channel_id=1, replica_groups={{192,200,80,88,32,40,176,184},{193,201,81,89,33,41,177,185},{194,202,82..., dimensions={0} | all-to-all | bytes 786432 | tf_op jit(solution)/shard_map/all_to_all | solution.py:282
  25.5 0.0 copy-start.1
  25.5 0.1 broadcast_in_dim.4
  25.6 11.5 %all_to_all.21 = bf16[4,8,64,128]{3,2,1,0:T(8,128)(2,1)S(1)} all-to-all(bf16[4,8,64,128]{3,2,1,0:T(8,128)(2,1)S(1)} %broadcast_in_dim.4), channel_id=1, replica_groups={{0,64,128,192},{1,65,129,193},{2,66,130,194},{3,67,131,195},{4,5,6,7},{..., dimensions={0} | all-to-all | bytes 1048576 | tf_op jit(solution)/shard_map/all_to_all | solution.py:286
  37.1 0.5 broadcast_in_dim.5
  37.6 0.0 copy-done.1
  37.6 0.0 copy-start
  37.6 20.9 %all_to_all.22 = bf16[4,4,8,64,128]{4,3,2,1,0:T(8,128)(2,1)} all-to-all(bf16[4,4,8,64,128]{4,3,2,1,0:T(8,128)(2,1)S(1)} %broadcast_in_dim.5), channel_id=1, replica_groups={{0,1,2,3},{64,65,66,67},{128,129,130,131},{192,193,194,195},{4,68,132,1..., dimensions={0} | all-to-all | bytes 4194304 | tf_op jit(solution)/shard_map/all_to_all | solution.py:286
  58.5 0.0 collective-permute-start
  58.5 3.2 %attention_start.1 = (bf16[4,128,512]{2,1,0:T(8,128)(2,1)S(1)}, f32[4,1,512]{2,1,0:T(1,128)S(1)}, f32[4,128,512]{2,1,0:T(8,128)S(1)}) custom-call(s32[17]{0:T(128)} %bounds.5, bf16[8,64,384]{2,1,0:T(8,128)(2,1)} %copy-done.1), custom_call_target="tpu_custom_call" | custom-call | tf_op jit(solution)/shard_map/attention_start/pallas_call | solution.py:294
  61.7 0.0 copy-done
  61.7 7.1 %attention_own.1.refs_2_ = f32[4,128,512]{2,1,0:T(8,128)S(1)} custom-call(s32[17]{0:T(128)S(1)} %copy-done, bf16[4,128,512]{2,1,0:T(8,128)(2,1)S(1)} %get-tuple-element.8.refs_0_, f32[4,1,512]{2,1,0:T(1,128)S(1)} %get-tuple-element.9.refs_1_, f32[4,128,512]{2,1,0:T(8,128)S(1)} %get-tuple-element.10.refs_2_, bf16[16,8,64,128]{3,2,1,0:T(8,128)(2,1)} %bitcast.refs_3_), custom_call_target="tpu_custom_call" | custom-call | tf_op jit(solution)/shard_map/attention_own/pallas_call | solution.py:301
  68.8 0.0 collective-permute-done.refs_4_
  68.8 8.6 %attention_other.1 = bf16[8,64,256]{2,1,0:T(8,128)(2,1)S(1)} custom-call(s32[17]{0:T(128)S(1)} %copy-done, bf16[4,128,512]{2,1,0:T(8,128)(2,1)S(1)} %get-tuple-element.8.refs_0_, f32[4,1,512]{2,1,0:T(1,128)S(1)} %get-tuple-element.9.refs_1_, f32[4,128,512]{2,1,0:T(8,128)S(1)} %attention_own.1.refs_2_, bf16[16,8,64,128]{3,2,1,0:T(8,128)(2,1)} %bitcast.refs_3_, ...), custom_call_target="tpu_custom_call" | custom-call | tf_op jit(solution)/shard_map/attention_other/pallas_call | solution.py:309
  77.4 18.3 %all_to_all.23 = bf16[8,64,256]{2,1,0:T(8,128)(2,1)S(1)} all-to-all(bf16[8,64,256]{2,1,0:T(8,128)(2,1)S(1)} %attention_other.1), channel_id=1, replica_groups={{192,200,80,88,32,40,176,184},{193,201,81,89,33,41,177,185},{194,202,82..., dimensions={0} | all-to-all | bytes 524288 | tf_op jit(solution)/shard_map/all_to_all | solution.py:318
  95.7 0.7 copy.6
  (1 shorter events, 0.0 us)
Async XLA Ops:
  25.5 12.1 %copy-start.1 = (bf16[8,64,384]{2,1,0:T(8,128)(2,1)}, bf16[8,64,384]{2,1,0:T(8,128)(2,1)S(1)}, u32[]{:S(2)}) copy-start(bf16[8,64,384]{2,1,0:T(8,128)(2,1)S(1)} %all_to_all.20.q_ref) | copy-start | bytes 1179652
  37.6 24.1 %copy-start = (s32[17]{0:T(128)S(1)}, s32[17]{0:T(128)}, u32[]{:S(2)}) copy-start(s32[17]{0:T(128)} %bounds.5) | copy-start | bytes 208
  58.5 10.3 %collective-permute-start = (bf16[16,8,64,128]{3,2,1,0:T(8,128)(2,1)}, bf16[16,8,64,128]{3,2,1,0:T(8,128)(2,1)}, u32[]{:S(2)}, u32[]{:S(2)}) collective-permute-start(bf16[16,8,64,128]{3,2,1,0:T(8,128)(2,1)} %bitcast.refs_3_), channel_id=1, source_target_pairs={{0,4},{4,0},{1,5},{5,1},{2,6},{6,2},{3,7},{7,3},{8,12},{12,8},{9,1... | collective-permute-start | bytes 6291464 | tf_op jit(solution)/shard_map/ppermute | solution.py:288
where the time goes:
time: 96.7 us; the launch traced here: 96.4 us
  blocking collectives  75 us (78%)
  Pallas kernels  20 us (21%)
  local copies, waits for them, and re-layouts  1.38 us (1%)
    all_to_all x2, blocking collectives, on_device(): lax.all_to_all(copies, AXES, 0, 0, axis_index_groups=line_groups(first),...  32.3 us
    all_to_all x1, blocking collectives, on_device(): lax.all_to_all(packed, AXES, 0, 0, axis_index_groups=groups, tiled=True)  24.4 us
    all_to_all x1, blocking collectives, on_device(): lax.all_to_all(attended, AXES, 0, 0, axis_index_groups=groups, tiled=True)  18.3 us
    pallas_call x1, Pallas kernels, on_device(): pl.pallas_call(functools.partial(attention_kernel, 1), out_shape=jax.Shap...  8.58 us
    pallas_call x1, Pallas kernels, on_device(): pl.pallas_call(functools.partial(attention_kernel, 0), out_shape=acc_shap...  7.08 us
    pallas_call x1, Pallas kernels, on_device(): pl.pallas_call(start_kernel, out_shape=tuple((pltpu.VMEM(a.shape, a.dtype...  3.19 us
  transfers between devices with their start and end apart: 1, of which 0 were waited for; matrix products, arithmetic and copies ran while one was open for 0% of the time, Pallas kernels for 11%

commit v1 on v0

--- a/solution.py
+++ b/solution.py
@@ -60,7 +60,7 @@
     groups = []
     for z in range(Z):
         for core in range(CORES):
-            if (core == 0) == first:
+            if (core == 1) == first:
                 groups += [[index(x, z, core, y) for x in range(X)] for y in range(Y)]
             else:
                 groups += [[index(x, z, core, y) for y in range(Y)] for x in range(X)]
@@ -149,7 +149,7 @@
                 source = lax.div(near, PAIRS) ^ base_of(q) ^ mine
                 for g in range(PAIR):
                     for i in range(Y):
-                        at = jnp.where(offset == 0, i * X + source, source * Y + i)
+                        at = jnp.where(offset == 1, i * X + source, source * Y + i)
                         parts.append(kv_ref[at, q * PAIR + g])
                 origin = block * STRIDE + offset * TILE
                 origins.append(origin)
@@ -193,21 +193,33 @@
 
         @pl.when(one_document)
         def _():
-            add([home, begin], [start, jnp.where(begin == home, NEVER, start)])
             inside = home - begin - 1
+            many = inside >= 2
+
+            @pl.when(many)
+            def _():
+                add([home, begin, begin + 1, begin + 2], [start] * 4)
+
+            @pl.when(jnp.logical_not(many))
+            def _():
+                add([home, begin], [start, jnp.where(begin == home, NEVER, start)])
+
+            taken = jnp.where(many, 2, 0)
+            left = inside - taken
+            base = begin + 1 + taken
 
             def step(s, _):
-                add([begin + 1 + 4 * s + n for n in range(4)])
+                add([base + 4 * s + n for n in range(4)])
                 return 0
 
-            lax.fori_loop(0, lax.div(inside, 4), step, 0)
-
-            @pl.when((inside > 0) & (lax.rem(inside, 4) >= 2))
-            def _():
-                left = begin + 1 + inside - lax.rem(inside, 4)
-                add([left, left + 1])
-
-            @pl.when((inside > 0) & (lax.rem(inside, 2) == 1))
+            lax.fori_loop(0, lax.div(left, 4), step, 0)
+
+            @pl.when((left > 0) & (lax.rem(left, 4) >= 2))
+            def _():
+                at = base + left - lax.rem(left, 4)
+                add([at, at + 1])
+
+            @pl.when((left > 0) & (lax.rem(left, 2) == 1))
             def _():
                 add([home - 1])
 

time: 96.7 us -> 96.7 us (level)
  no operation moved by 1% of the time
where the time goes in v1:
time: 96.7 us; the launch traced here: 96.3 us
  blocking collectives  75 us (78%)
  Pallas kernels  19.8 us (20%)
  local copies, waits for them, and re-layouts  1.38 us (1%)
    all_to_all x2, blocking collectives, on_device(): lax.all_to_all(copies, AXES, 0, 0, axis_index_groups=line_groups(first),...  33.1 us
    all_to_all x1, blocking collectives, on_device(): lax.all_to_all(packed, AXES, 0, 0, axis_index_groups=groups, tiled=True)  24.4 us
    all_to_all x1, blocking collectives, on_device(): lax.all_to_all(attended, AXES, 0, 0, axis_index_groups=groups, tiled=True)  17.6 us
    pallas_call x1, Pallas kernels, on_device(): pl.pallas_call(functools.partial(attention_kernel, 1), out_shape=jax.Shap...  8.46 us
    pallas_call x1, Pallas kernels, on_device(): pl.pallas_call(functools.partial(attention_kernel, 0), out_shape=acc_shap...  7.08 us
    pallas_call x1, Pallas kernels, on_device(): pl.pallas_call(start_kernel, out_shape=tuple((pltpu.VMEM(a.shape, a.dtype...  3.19 us
  transfers between devices with their start and end apart: 1, of which 0 were waited for; matrix products, arithmetic and copies ran while one was open for 0% of the time, Pallas kernels for 11%

profile of v1, /device:TPU:6, one launch (start us, length us, event | category | flops | bytes accessed | tf_op | source)
XLA Modules:
  0.0 96.3 jit_solution(11298379241217626802)
XLA Ops:
  0.0 1.1 %pack.1 = bf16[8,64,384]{2,1,0:T(8,128)(2,1)S(1)} custom-call(bf16[64,2048]{1,0:T(8,128)(2,1)} %q_ref.1, bf16[64,512]{1,0:T(8,128)(2,1)} %k_ref.1, bf16[64,512]{1,0:T(8,128)(2,1)} %v_ref.1), custom_call_target="tpu_custom_call" | custom-call | tf_op jit(solution)/shard_map/pack/pallas_call | solution.py:287
  1.1 24.4 %all_to_all.20.q_ref = bf16[8,64,384]{2,1,0:T(8,128)(2,1)S(1)} all-to-all(bf16[8,64,384]{2,1,0:T(8,128)(2,1)S(1)} %pack.1), channel_id=1, replica_groups={{192,200,80,88,32,40,176,184},{193,201,81,89,33,41,177,185},{194,202,82..., dimensions={0} | all-to-all | bytes 786432 | tf_op jit(solution)/shard_map/all_to_all | solution.py:294
  25.5 0.0 copy-start.1
  25.5 0.1 broadcast_in_dim.4
  25.6 12.3 %all_to_all.21 = bf16[4,8,64,128]{3,2,1,0:T(8,128)(2,1)S(1)} all-to-all(bf16[4,8,64,128]{3,2,1,0:T(8,128)(2,1)S(1)} %broadcast_in_dim.4), channel_id=1, replica_groups={{0,1,2,3},{64,65,66,67},{128,129,130,131},{192,193,194,195},{4,68,132,1..., dimensions={0} | all-to-all | bytes 1048576 | tf_op jit(solution)/shard_map/all_to_all | solution.py:298
  38.0 0.5 broadcast_in_dim.5
  38.5 0.0 copy-done.1
  38.5 0.0 copy-start
  38.5 20.7 %all_to_all.22 = bf16[4,4,8,64,128]{4,3,2,1,0:T(8,128)(2,1)} all-to-all(bf16[4,4,8,64,128]{4,3,2,1,0:T(8,128)(2,1)S(1)} %broadcast_in_dim.5), channel_id=1, replica_groups={{0,64,128,192},{1,65,129,193},{2,66,130,194},{3,67,131,195},{4,5,6,7},{..., dimensions={0} | all-to-all | bytes 4194304 | tf_op jit(solution)/shard_map/all_to_all | solution.py:298
  59.2 0.0 collective-permute-start
  59.2 3.2 %attention_start.1 = (bf16[4,128,512]{2,1,0:T(8,128)(2,1)S(1)}, f32[4,1,512]{2,1,0:T(1,128)S(1)}, f32[4,128,512]{2,1,0:T(8,128)S(1)}) custom-call(s32[17]{0:T(128)} %bounds.5, bf16[8,64,384]{2,1,0:T(8,128)(2,1)} %copy-done.1), custom_call_target="tpu_custom_call" | custom-call | tf_op jit(solution)/shard_map/attention_start/pallas_call | solution.py:306
  62.4 0.0 copy-done
  62.4 7.1 %attention_own.1.refs_2_ = f32[4,128,512]{2,1,0:T(8,128)S(1)} custom-call(s32[17]{0:T(128)S(1)} %copy-done, bf16[4,128,512]{2,1,0:T(8,128)(2,1)S(1)} %get-tuple-element.8.refs_0_, f32[4,1,512]{2,1,0:T(1,128)S(1)} %get-tuple-element.9.refs_1_, f32[4,128,512]{2,1,0:T(8,128)S(1)} %get-tuple-element.10.refs_2_, bf16[16,8,64,128]{3,2,1,0:T(8,128)(2,1)} %bitcast.refs_3_), custom_call_target="tpu_custom_call" | custom-call | tf_op jit(solution)/shard_map/attention_own/pallas_call | solution.py:313
  69.5 0.0 collective-permute-done.refs_4_
  69.5 8.5 %attention_other.1 = bf16[8,64,256]{2,1,0:T(8,128)(2,1)S(1)} custom-call(s32[17]{0:T(128)S(1)} %copy-done, bf16[4,128,512]{2,1,0:T(8,128)(2,1)S(1)} %get-tuple-element.8.refs_0_, f32[4,1,512]{2,1,0:T(1,128)S(1)} %get-tuple-element.9.refs_1_, f32[4,128,512]{2,1,0:T(8,128)S(1)} %attention_own.1.refs_2_, bf16[16,8,64,128]{3,2,1,0:T(8,128)(2,1)} %bitcast.refs_3_, ...), custom_call_target="tpu_custom_call" | custom-call | tf_op jit(solution)/shard_map/attention_other/pallas_call | solution.py:321
  78.0 17.6 %all_to_all.23 = bf16[8,64,256]{2,1,0:T(8,128)(2,1)S(1)} all-to-all(bf16[8,64,256]{2,1,0:T(8,128)(2,1)S(1)} %attention_other.1), channel_id=1, replica_groups={{192,200,80,88,32,40,176,184},{193,201,81,89,33,41,177,185},{194,202,82..., dimensions={0} | all-to-all | bytes 524288 | tf_op jit(solution)/shard_map/all_to_all | solution.py:330
  95.6 0.7 copy.6
  (1 shorter events, 0.0 us)
Async XLA Ops:
  25.5 13.0 %copy-start.1 = (bf16[8,64,384]{2,1,0:T(8,128)(2,1)}, bf16[8,64,384]{2,1,0:T(8,128)(2,1)S(1)}, u32[]{:S(2)}) copy-start(bf16[8,64,384]{2,1,0:T(8,128)(2,1)S(1)} %all_to_all.20.q_ref) | copy-start | bytes 1179652
  38.5 23.9 %copy-start = (s32[17]{0:T(128)S(1)}, s32[17]{0:T(128)}, u32[]{:S(2)}) copy-start(s32[17]{0:T(128)} %bounds.5) | copy-start | bytes 208
  59.2 10.3 %collective-permute-start = (bf16[16,8,64,128]{3,2,1,0:T(8,128)(2,1)}, bf16[16,8,64,128]{3,2,1,0:T(8,128)(2,1)}, u32[]{:S(2)}, u32[]{:S(2)}) collective-permute-start(bf16[16,8,64,128]{3,2,1,0:T(8,128)(2,1)} %bitcast.refs_3_), channel_id=1, source_target_pairs={{0,4},{4,0},{1,5},{5,1},{2,6},{6,2},{3,7},{7,3},{8,12},{12,8},{9,1... | collective-permute-start | bytes 6291464 | tf_op jit(solution)/shard_map/ppermute | solution.py:300

commit v2 on v1

--- a/solution.py
+++ b/solution.py
@@ -28,6 +28,8 @@
 ROWS = PAIR * HALF
 KEYS = PAIR * TILE
 WIDE = 2 * HEAD_SIZE
+SUMS = 16
+MIXED = SUMS + HEAD_SIZE
 HEAD_COLS = GROUP * HEAD_SIZE
 BASE = (3, 1, 0, 2)
 BLOCKS = X * PAIRS
@@ -107,7 +109,7 @@
         scores = jnp.where((k_offset >= lo) & (k_offset <= row_offset), scores, HIDDEN)
         top = jnp.max(scores, axis=0, keepdims=True)
         top_ref[p] = top
-        acc_ref[p] = mix((kv * value_lanes + key_lanes).T, jnp.exp2(scores * EXP2_SCALE - top * EXP2_SCALE))
+        acc_ref[p] = mix((kv * value_lanes + key_lanes).T[WIDE - MIXED:], jnp.exp2(scores * EXP2_SCALE - top * EXP2_SCALE))
         return 0
 
     lax.fori_loop(0, PAIRS, one_pair, 0)
@@ -163,7 +165,7 @@
             keys = kv * key_lanes
             if limits is not None:
                 keys = keys + jnp.concatenate(masks, axis=0).astype(jnp.bfloat16)
-            return keys, (kv * value_lanes + key_lanes).T, origins
+            return keys, (kv * value_lanes + key_lanes).T[WIDE - MIXED:], origins
 
         def across(origins, low, high=None):
             offsets = jnp.concatenate([key_offset] * (ROWS // WIDE), axis=1)
@@ -264,7 +266,7 @@
 
                 lax.fori_loop(begin, home + 1, step, 0)
 
-        result = (acc[HEAD_SIZE:, :] / acc[0:1, :]).T
+        result = (acc[SUMS:, :] / acc[0:1, :]).T
         for b in range(PAIR):
             heads = [result[(b * GROUP + j) * BLOCK:(b * GROUP + j + 1) * BLOCK] for j in range(GROUP)]
             out_ref[PAIR * p + b] = jnp.concatenate(heads, axis=1).astype(jnp.bfloat16)
@@ -299,7 +301,7 @@
     own = gathered.reshape(X * Y, Z, BLOCK, WIDE)
     other = lax.ppermute(own, "core", [(0, 1), (1, 0)])
 
-    acc_shape = jax.ShapeDtypeStruct((PAIRS, WIDE, ROWS), jnp.float32)
+    acc_shape = jax.ShapeDtypeStruct((PAIRS, MIXED, ROWS), jnp.float32)
     top_shape = jax.ShapeDtypeStruct((PAIRS, 1, ROWS), jnp.float32)
     rows_shape = jax.ShapeDtypeStruct((PAIRS, WIDE, ROWS), jnp.bfloat16)
     params = pltpu.CompilerParams(vmem_limit_bytes=40 * 1024 * 1024)
@@ -323,7 +325,7 @@
         out_shape=jax.ShapeDtypeStruct((Z, BLOCK, HEAD_COLS), jnp.bfloat16),
         in_specs=[smem] + [vmem] * 5,
         out_specs=vmem,
-        scratch_shapes=[pltpu.VMEM((WIDE, ROWS), jnp.float32), pltpu.VMEM((1, ROWS), jnp.float32)],
+        scratch_shapes=[pltpu.VMEM((MIXED, ROWS), jnp.float32), pltpu.VMEM((1, ROWS), jnp.float32)],
         compiler_params=params,
         name="attention_other",
     )(doc_bounds, rows, top, acc, own, other)

time: 96.7 us -> 95.4 us (0.987)
  Pallas kernels: 19.8 us -> 18.1 us
    pallas_call x1, Pallas kernels: 7.08 us -> 6.1 us  [on_device(): pl.pallas_call(functools.partial(attention_kernel, 0), out_shape=acc_shap...]
  transfers between devices with their start and end apart: 1 -> 1, of which waited for: 0 -> 0; matrix products, arithmetic and copies ran while one was open for 0% -> 0% of each run, Pallas kernels for 11% -> 10%
where the time goes in v2:
time: 95.4 us; the launch traced here: 95.1 us
  blocking collectives  74.8 us (78%)
  Pallas kernels  18.1 us (19%)
  local copies, waits for them, and re-layouts  2.12 us (2%)
    all_to_all x2, blocking collectives, on_device(): lax.all_to_all(copies, AXES, 0, 0, axis_index_groups=line_groups(first),...  32.3 us
    all_to_all x1, blocking collectives, on_device(): lax.all_to_all(packed, AXES, 0, 0, axis_index_groups=groups, tiled=True)  24.4 us
    all_to_all x1, blocking collectives, on_device(): lax.all_to_all(attended, AXES, 0, 0, axis_index_groups=groups, tiled=True)  18.1 us
    pallas_call x1, Pallas kernels, on_device(): pl.pallas_call(functools.partial(attention_kernel, 1), out_shape=jax.Shap...  7.81 us
    pallas_call x1, Pallas kernels, on_device(): pl.pallas_call(functools.partial(attention_kernel, 0), out_shape=acc_shap...  6.1 us
    pallas_call x1, Pallas kernels, on_device(): pl.pallas_call(start_kernel, out_shape=tuple((pltpu.VMEM(a.shape, a.dtype...  3.14 us
  transfers between devices with their start and end apart: 1, of which 0 were waited for; matrix products, arithmetic and copies ran while one was open for 0% of the time, Pallas kernels for 10%

profile of v2, /device:TPU:6, one launch (start us, length us, event | category | flops | bytes accessed | tf_op | source)
XLA Modules:
  0.0 95.1 jit_solution(11776135303840035877)
XLA Ops:
  0.0 1.1 %pack.1 = bf16[8,64,384]{2,1,0:T(8,128)(2,1)S(1)} custom-call(bf16[64,2048]{1,0:T(8,128)(2,1)} %q_ref.1, bf16[64,512]{1,0:T(8,128)(2,1)} %k_ref.1, bf16[64,512]{1,0:T(8,128)(2,1)} %v_ref.1), custom_call_target="tpu_custom_call" | custom-call | tf_op jit(solution)/shard_map/pack/pallas_call | solution.py:289
  1.1 24.4 %all_to_all.20.q_ref = bf16[8,64,384]{2,1,0:T(8,128)(2,1)S(1)} all-to-all(bf16[8,64,384]{2,1,0:T(8,128)(2,1)S(1)} %pack.1), channel_id=1, replica_groups={{192,200,80,88,32,40,176,184},{193,201,81,89,33,41,177,185},{194,202,82..., dimensions={0} | all-to-all | bytes 786432 | tf_op jit(solution)/shard_map/all_to_all | solution.py:296
  25.5 0.0 copy-start.1
  25.5 0.7 copy-done.1
  26.3 0.1 broadcast_in_dim.4
  26.4 12.3 %all_to_all.21 = bf16[4,8,64,128]{3,2,1,0:T(8,128)(2,1)S(1)} all-to-all(bf16[4,8,64,128]{3,2,1,0:T(8,128)(2,1)S(1)} %broadcast_in_dim.4), channel_id=1, replica_groups={{0,1,2,3},{64,65,66,67},{128,129,130,131},{192,193,194,195},{4,68,132,1..., dimensions={0} | all-to-all | bytes 1048576 | tf_op jit(solution)/shard_map/all_to_all | solution.py:300
  38.7 0.5 broadcast_in_dim.5
  39.2 0.0 copy-start
  39.3 19.9 %all_to_all.22 = bf16[4,4,8,64,128]{4,3,2,1,0:T(8,128)(2,1)S(1)} all-to-all(bf16[4,4,8,64,128]{4,3,2,1,0:T(8,128)(2,1)S(1)} %broadcast_in_dim.5), channel_id=1, replica_groups={{0,64,128,192},{1,65,129,193},{2,66,130,194},{3,67,131,195},{4,5,6,7},{..., dimensions={0} | all-to-all | bytes 4194304 | tf_op jit(solution)/shard_map/all_to_all | solution.py:300
  59.2 0.0 collective-permute-start
  59.2 3.1 %attention_start.1 = (bf16[4,128,512]{2,1,0:T(8,128)(2,1)S(1)}, f32[4,1,512]{2,1,0:T(1,128)S(1)}, f32[4,80,512]{2,1,0:T(8,128)S(1)}) custom-call(s32[17]{0:T(128)} %bounds.5, bf16[8,64,384]{2,1,0:T(8,128)(2,1)} %copy-done.1), custom_call_target="tpu_custom_call" | custom-call | tf_op jit(solution)/shard_map/attention_start/pallas_call | solution.py:308
  62.3 0.0 copy-done
  62.4 6.1 %attention_own.1.refs_2_ = f32[4,80,512]{2,1,0:T(8,128)S(1)} custom-call(s32[17]{0:T(128)S(1)} %copy-done, bf16[4,128,512]{2,1,0:T(8,128)(2,1)S(1)} %get-tuple-element.8.refs_0_, f32[4,1,512]{2,1,0:T(1,128)S(1)} %get-tuple-element.9.refs_1_, f32[4,80,512]{2,1,0:T(8,128)S(1)} %get-tuple-element.10.refs_2_, bf16[16,8,64,128]{3,2,1,0:T(8,128)(2,1)S(1)} %bitcast.5), custom_call_target="tpu_custom_call" | custom-call | tf_op jit(solution)/shard_map/attention_own/pallas_call | solution.py:315
  68.5 0.0 collective-permute-done.refs_4_
  68.5 7.8 %attention_other.1 = bf16[8,64,256]{2,1,0:T(8,128)(2,1)S(1)} custom-call(s32[17]{0:T(128)S(1)} %copy-done, bf16[4,128,512]{2,1,0:T(8,128)(2,1)S(1)} %get-tuple-element.8.refs_0_, f32[4,1,512]{2,1,0:T(1,128)S(1)} %get-tuple-element.9.refs_1_, f32[4,80,512]{2,1,0:T(8,128)S(1)} %attention_own.1.refs_2_, bf16[16,8,64,128]{3,2,1,0:T(8,128)(2,1)S(1)} %bitcast.6, ...), custom_call_target="tpu_custom_call" | custom-call | tf_op jit(solution)/shard_map/attention_other/pallas_call | solution.py:323
  76.3 18.1 %all_to_all.23 = bf16[8,64,256]{2,1,0:T(8,128)(2,1)S(1)} all-to-all(bf16[8,64,256]{2,1,0:T(8,128)(2,1)S(1)} %attention_other.1), channel_id=1, replica_groups={{192,200,80,88,32,40,176,184},{193,201,81,89,33,41,177,185},{194,202,82..., dimensions={0} | all-to-all | bytes 524288 | tf_op jit(solution)/shard_map/all_to_all | solution.py:332
  94.4 0.7 copy.6
  (1 shorter events, 0.0 us)
Async XLA Ops:
  25.5 0.7 copy-start.1
  39.2 23.1 %copy-start = (s32[17]{0:T(128)S(1)}, s32[17]{0:T(128)}, u32[]{:S(2)}) copy-start(s32[17]{0:T(128)} %bounds.5) | copy-start | bytes 208
  59.2 9.3 %collective-permute-start = (bf16[16,8,64,128]{3,2,1,0:T(8,128)(2,1)S(1)}, bf16[16,8,64,128]{3,2,1,0:T(8,128)(2,1)}, u32[]{:S(2)}, u32[]{:S(2)}) collective-permute-start(bf16[16,8,64,128]{3,2,1,0:T(8,128)(2,1)S(1)} %bitcast.4), channel_id=1, source_target_pairs={{0,4},{4,0},{1,5},{5,1},{2,6},{6,2},{3,7},{7,3},{8,12},{12,8},{9,1... | collective-permute-start | bytes 6291464 | tf_op jit(solution)/shard_map/ppermute | solution.py:302
